TPU v7x, 32 devices: a whole 2x2x4 slice. The times are simulated.
32 devices in a mesh: blk: 8 (over y, x, core), wide: 4 (over z).
Axes of the slice: x: 2, y: 2, z: 4, core: 2. Of those that a mesh axis runs over, the one named last changes fastest.
Arguments:
- points: bfloat16 [8192, 32], P(('blk', 'wide')), may hold values from -6 to 6
- inv_length: float32 [32], replicated, may hold values from 0.2 to 0.7
- noise_var: float32 [], replicated, may hold values from 0.1 to 1
- solution: float32 [8192, 128], P(('blk', 'wide')), may hold values from -6 to 6
- residual: float32 [8192, 128], P(('blk', 'wide')), may hold values from -6 to 6
- direction: float32 [8192, 128], P(('blk', 'wide')), may hold values from -6 to 6
Outputs:
- new_solution: float32 [8192, 128], P(('blk', 'wide'))
- new_residual: float32 [8192, 128], P(('blk', 'wide'))
- new_direction: float32 [8192, 128], P(('blk', 'wide'))
All inputs are finite; a program needn't handle non-finite values.
Results may differ from a plain program's by a relative error of at most 0.01.
Values may be sent and summed in bfloat16 or wider, within the bound.
A program may use at most 64 MiB of HBM per device.

v0:
```python
import jax
import jax.numpy as jnp
from jax import lax
from jax.sharding import PartitionSpec as P


def shifted(x, axis, by):
    count = lax.axis_size(axis)
    return lax.ppermute(x, axis, [(i, (i + by) % count) for i in range(count)])


def squares_of(values):
    wide_values = values.astype(jnp.float32)
    return jnp.sum(wide_values * wide_values, axis=1)


def kernel_tile(rows_x, rows_sq, cols_x, cols_sq):
    inner_prod = lax.dot_general(
        rows_x, cols_x, (((1,), (1,)), ((), ())), preferred_element_type=jnp.float32
    )
    dist_sq = jnp.maximum(rows_sq[:, None] + cols_sq[None, :] - 2.0 * inner_prod, 0.0)
    radius = jnp.sqrt(5.0 * dist_sq)
    return ((1.0 + radius + radius * radius / 3.0) * jnp.exp(-radius)).astype(jnp.bfloat16)


def on_device(points, inv_length, noise_var, solution, residual, direction):
    scaled = (points.astype(jnp.float32) * inv_length).astype(jnp.bfloat16)
    low_dir = direction.astype(jnp.bfloat16)
    own_sq = squares_of(scaled)
    block_x, block_p = (
        lax.all_gather(scaled, "wide", axis=0, tiled=True),
        lax.all_gather(low_dir, "wide", axis=0, tiled=True),
    )
    block_sq = squares_of(block_x)
    cycle_size = lax.axis_size("blk")
    row_sums = jnp.dot(
        kernel_tile(block_x, block_sq, scaled, own_sq), low_dir, preferred_element_type=jnp.float32
    )

    def direct_turn(counter, carried):
        piece_x, piece_p, row_total = carried
        piece_x, piece_p = shifted((piece_x, piece_p), "blk", 1)
        kernel_block = kernel_tile(block_x, block_sq, piece_x, squares_of(piece_x))
        row_total = row_total + jnp.dot(kernel_block, piece_p, preferred_element_type=jnp.float32)
        return (piece_x, piece_p, row_total)

    result = lax.fori_loop(0, cycle_size - 1, direct_turn, (scaled, low_dir, row_sums))
    own_image = lax.psum_scatter(result[2], "wide", scatter_dimension=0, tiled=True)
    kernel_image = own_image + noise_var * direction
    old_norm, curvature, cross_term, image_norm = lax.psum(
        (
            jnp.sum(residual * residual, axis=0),
            jnp.sum(direction * kernel_image, axis=0),
            jnp.sum(residual * kernel_image, axis=0),
            jnp.sum(kernel_image * kernel_image, axis=0),
        ),
        ("blk", "wide"),
    )
    step_length = old_norm / curvature
    new_residual = residual - step_length * kernel_image
    new_norm = old_norm - 2.0 * step_length * cross_term + step_length * step_length * image_norm
    new_solution = solution + step_length * direction
    new_direction = new_residual + new_norm / old_norm * direction
    return (new_solution, new_residual, new_direction)


def solution(mesh):
    return jax.shard_map(
        on_device,
        mesh=mesh,
        in_specs=(
            P(("blk", "wide"), None),
            P(),
            P(),
            P(("blk", "wide"), None),
            P(("blk", "wide"), None),
            P(("blk", "wide"), None),
        ),
        out_specs=(P(("blk", "wide"), None), P(("blk", "wide"), None), P(("blk", "wide"), None)),
        check_vma=False,
    )
```

profile of v0, /device:TPU:0, one launch (start us, length us, event | category | flops | bytes accessed | tf_op | source)
XLA Modules:
  0.0 140.3 jit_solution(16337664160268755583)
XLA Ops:
  7.2 0.8 copy.9
  8.1 0.1 multiply_reduce_fusion.5
  8.2 15.7 %all_gather.3 = bf16[1024,32]{1,0:T(8,128)(2,1)S(1)} all-gather(bf16[256,32]{1,0:T(8,128)(2,1)S(1)} %get-tuple-element.102), channel_id=1, replica_groups=mesh['blk'=8,'wide'=4] {'wide'}, dimensions={0}, use_global_device_ids=true | all-gather | bytes 81920 | tf_op jit(solution)/shard_map/all_gather | solution.py:31
  23.8 0.2 multiply_reduce_fusion.1
  24.1 0.7 copy-done
  24.8 0.9 fusion.16
  25.7 44.2 %while.14 = (s32[]{:T(128)}, bf16[256,32]{1,0:T(8,128)(2,1)S(1)}, bf16[256,128]{1,0:T(8,128)(2,1)S(1)}, f32[1024,128]{1,0:T(8,128)S(1)}, f32[1024]{0:T(1024)S(1)}, /*index=5*/bf16[1024,32]{1,0:T(8,128)(2,1)S(1)}, s32[]{:T(128)}) while((s32[]{:T(128)}, bf16[256,32]{1,0:T(8,128)(2,1)S(1)}, bf16[256,128]{1,0:T(8,128)(2,1)S(1)}, ...), condition=%wide.region_6.0_spmd, body=%wide.region_4.6_spmd.sunk | while | flops 87187200 | bytes 1710237 | solution.py:47
  25.7 0.1 collective-permute-start
  25.8 1.6 %collective-permute-start.1 = (bf16[256,128]{1,0:T(8,128)(2,1)S(1)}, bf16[256,128]{1,0:T(8,128)(2,1)S(1)}, u32[]{:S(2)}, u32[]{:S(2)}) collective-permute-start(bf16[256,128]{1,0:T(8,128)(2,1)S(1)} %get-tuple-element.110), channel_id=1, source_target_pairs={{0,4},{4,8},{8,12},{12,16},{16,20},{20,24},{24,28},{28,0},{1,5},{5... | collective-permute-start | bytes 196616 | tf_op jit(solution)/shard_map/while/body/eval_jaxpr/ppermute | solution.py:9
  27.4 3.0 %collective-permute-done = bf16[256,32]{1,0:T(8,128)(2,1)S(1)} collective-permute-done((bf16[256,32]{1,0:T(8,128)(2,1)S(1)}, bf16[256,32]{1,0:T(8,128)(2,1)S(1)}, u32[]{:S(2)}, u32[]{:S(2)}) %collective-permute-start) | collective-permute-done | bytes 16416 | tf_op jit(solution)/shard_map/while/body/eval_jaxpr/ppermute | solution.py:9
  30.3 0.1 multiply_reduce_fusion.8
  30.5 0.6 collective-permute-done.1
  31.0 1.0 convolution_add_fusion.2
  32.0 0.1 collective-permute-start
  32.1 0.7 collective-permute-start.1
  32.8 3.9 %collective-permute-done = bf16[256,32]{1,0:T(8,128)(2,1)S(1)} collective-permute-done((bf16[256,32]{1,0:T(8,128)(2,1)S(1)}, bf16[256,32]{1,0:T(8,128)(2,1)S(1)}, u32[]{:S(2)}, u32[]{:S(2)}) %collective-permute-start) | collective-permute-done | bytes 16416 | tf_op jit(solution)/shard_map/while/body/eval_jaxpr/ppermute | solution.py:9
  36.6 0.1 multiply_reduce_fusion.8
  36.8 0.6 collective-permute-done.1
  37.4 1.0 convolution_add_fusion.2
  38.4 0.1 collective-permute-start.1
  38.4 4.5 %collective-permute-done = bf16[256,32]{1,0:T(8,128)(2,1)S(1)} collective-permute-done((bf16[256,32]{1,0:T(8,128)(2,1)S(1)}, bf16[256,32]{1,0:T(8,128)(2,1)S(1)}, u32[]{:S(2)}, u32[]{:S(2)}) %collective-permute-start) | collective-permute-done | bytes 16416 | tf_op jit(solution)/shard_map/while/body/eval_jaxpr/ppermute | solution.py:9
  43.0 0.1 multiply_reduce_fusion.8
  43.1 0.6 collective-permute-done.1
  43.7 1.0 convolution_add_fusion.2
  44.6 0.1 collective-permute-start
  44.7 4.5 %collective-permute-done = bf16[256,32]{1,0:T(8,128)(2,1)S(1)} collective-permute-done((bf16[256,32]{1,0:T(8,128)(2,1)S(1)}, bf16[256,32]{1,0:T(8,128)(2,1)S(1)}, u32[]{:S(2)}, u32[]{:S(2)}) %collective-permute-start) | collective-permute-done | bytes 16416 | tf_op jit(solution)/shard_map/while/body/eval_jaxpr/ppermute | solution.py:9
  49.3 0.1 multiply_reduce_fusion.8
  49.4 0.6 collective-permute-done.1
  50.0 1.0 convolution_add_fusion.2
  51.0 0.1 collective-permute-start.1
  51.1 4.5 %collective-permute-done = bf16[256,32]{1,0:T(8,128)(2,1)S(1)} collective-permute-done((bf16[256,32]{1,0:T(8,128)(2,1)S(1)}, bf16[256,32]{1,0:T(8,128)(2,1)S(1)}, u32[]{:S(2)}, u32[]{:S(2)}) %collective-permute-start) | collective-permute-done | bytes 16416 | tf_op jit(solution)/shard_map/while/body/eval_jaxpr/ppermute | solution.py:9
  55.6 0.1 multiply_reduce_fusion.8
  55.7 0.6 collective-permute-done.1
  56.3 1.0 convolution_add_fusion.2
  57.2 0.1 collective-permute-start
  57.4 4.5 %collective-permute-done = bf16[256,32]{1,0:T(8,128)(2,1)S(1)} collective-permute-done((bf16[256,32]{1,0:T(8,128)(2,1)S(1)}, bf16[256,32]{1,0:T(8,128)(2,1)S(1)}, u32[]{:S(2)}, u32[]{:S(2)}) %collective-permute-start) | collective-permute-done | bytes 16416 | tf_op jit(solution)/shard_map/while/body/eval_jaxpr/ppermute | solution.py:9
  61.9 0.1 multiply_reduce_fusion.8
  62.0 0.6 collective-permute-done.1
  62.6 1.0 convolution_add_fusion.2
  63.7 4.5 %collective-permute-done = bf16[256,32]{1,0:T(8,128)(2,1)S(1)} collective-permute-done((bf16[256,32]{1,0:T(8,128)(2,1)S(1)}, bf16[256,32]{1,0:T(8,128)(2,1)S(1)}, u32[]{:S(2)}, u32[]{:S(2)}) %collective-permute-start) | collective-permute-done | bytes 16416 | tf_op jit(solution)/shard_map/while/body/eval_jaxpr/ppermute | solution.py:9
  68.2 0.1 multiply_reduce_fusion.8
  68.3 0.6 collective-permute-done.1
  68.9 1.0 convolution_add_fusion.2
  69.9 0.8 copy-done.1
  71.3 22.0 %reduce-scatter.2.cloned.1.call-done = f32[256,128]{1,0:T(8,128)} async-done(((f32[1024,128]{1,0:T(8,128)}), f32[256,128]{1,0:T(8,128)}) %reduce-scatter.2.cloned.1.call-update) | async-done | bytes 131088 | tf_op jit(solution)/shard_map/reduce_scatter | solution.py:48
  93.3 1.0 multiply_reduce_fusion.3
  94.3 38.4 %all-reduce = (f32[128]{0:T(128)S(1)}, f32[128]{0:T(128)S(1)}, f32[128]{0:T(128)S(1)}, f32[128]{0:T(128)S(1)}) all-reduce(f32[128]{0:T(128)S(1)} %get-tuple-element.39, f32[128]{0:T(128)S(1)} %get-tuple-element.38, f32[128]{0:T(128)S(1)} %get-tuple-element.37, ...), channel_id=1, replica_groups=mesh['blk'=8,'wide'=4] {'blk','wide'}, use_global_device_ids=true, to_apply=%region_1.0 | all-reduce | flops 512 | bytes 4096 | tf_op jit(solution)/shard_map/psum | solution.py:50
  132.7 0.8 multiply_add_fusion
  (32 shorter events, 0.5 us)
Async XLA Ops:
  7.2 0.9 copy-start.4
  7.2 86.1 %reduce-scatter.2.cloned.1.call-start = ((), (), s32[]{:S(2)}) async-start(), calls=%async_computation.1 | async-start | bytes 655360 | tf_op jit(solution)/shard_map/reduce_scatter | solution.py:48
  23.8 0.9 copy-start
  25.7 4.6 %collective-permute-start = (bf16[256,32]{1,0:T(8,128)(2,1)S(1)}, bf16[256,32]{1,0:T(8,128)(2,1)S(1)}, u32[]{:S(2)}, u32[]{:S(2)}) collective-permute-start(bf16[256,32]{1,0:T(8,128)(2,1)S(1)} %get-tuple-element.109), channel_id=1, source_target_pairs={{0,4},{4,8},{8,12},{12,16},{16,20},{20,24},{24,28},{28,0},{1,5},{5... | collective-permute-start | bytes 49160 | tf_op jit(solution)/shard_map/while/body/eval_jaxpr/ppermute | solution.py:9
  25.8 5.3 %collective-permute-start.1 = (bf16[256,128]{1,0:T(8,128)(2,1)S(1)}, bf16[256,128]{1,0:T(8,128)(2,1)S(1)}, u32[]{:S(2)}, u32[]{:S(2)}) collective-permute-start(bf16[256,128]{1,0:T(8,128)(2,1)S(1)} %get-tuple-element.110), channel_id=1, source_target_pairs={{0,4},{4,8},{8,12},{12,16},{16,20},{20,24},{24,28},{28,0},{1,5},{5... | collective-permute-start | bytes 196616 | tf_op jit(solution)/shard_map/while/body/eval_jaxpr/ppermute | solution.py:9
  32.0 4.6 %collective-permute-start = (bf16[256,32]{1,0:T(8,128)(2,1)S(1)}, bf16[256,32]{1,0:T(8,128)(2,1)S(1)}, u32[]{:S(2)}, u32[]{:S(2)}) collective-permute-start(bf16[256,32]{1,0:T(8,128)(2,1)S(1)} %get-tuple-element.109), channel_id=1, source_target_pairs={{0,4},{4,8},{8,12},{12,16},{16,20},{20,24},{24,28},{28,0},{1,5},{5... | collective-permute-start | bytes 49160 | tf_op jit(solution)/shard_map/while/body/eval_jaxpr/ppermute | solution.py:9
  32.1 5.3 %collective-permute-start.1 = (bf16[256,128]{1,0:T(8,128)(2,1)S(1)}, bf16[256,128]{1,0:T(8,128)(2,1)S(1)}, u32[]{:S(2)}, u32[]{:S(2)}) collective-permute-start(bf16[256,128]{1,0:T(8,128)(2,1)S(1)} %get-tuple-element.110), channel_id=1, source_target_pairs={{0,4},{4,8},{8,12},{12,16},{16,20},{20,24},{24,28},{28,0},{1,5},{5... | collective-permute-start | bytes 196616 | tf_op jit(solution)/shard_map/while/body/eval_jaxpr/ppermute | solution.py:9
  38.3 4.6 %collective-permute-start = (bf16[256,32]{1,0:T(8,128)(2,1)S(1)}, bf16[256,32]{1,0:T(8,128)(2,1)S(1)}, u32[]{:S(2)}, u32[]{:S(2)}) collective-permute-start(bf16[256,32]{1,0:T(8,128)(2,1)S(1)} %get-tuple-element.109), channel_id=1, source_target_pairs={{0,4},{4,8},{8,12},{12,16},{16,20},{20,24},{24,28},{28,0},{1,5},{5... | collective-permute-start | bytes 49160 | tf_op jit(solution)/shard_map/while/body/eval_jaxpr/ppermute | solution.py:9
  38.4 5.3 %collective-permute-start.1 = (bf16[256,128]{1,0:T(8,128)(2,1)S(1)}, bf16[256,128]{1,0:T(8,128)(2,1)S(1)}, u32[]{:S(2)}, u32[]{:S(2)}) collective-permute-start(bf16[256,128]{1,0:T(8,128)(2,1)S(1)} %get-tuple-element.110), channel_id=1, source_target_pairs={{0,4},{4,8},{8,12},{12,16},{16,20},{20,24},{24,28},{28,0},{1,5},{5... | collective-permute-start | bytes 196616 | tf_op jit(solution)/shard_map/while/body/eval_jaxpr/ppermute | solution.py:9
  44.6 4.6 %collective-permute-start = (bf16[256,32]{1,0:T(8,128)(2,1)S(1)}, bf16[256,32]{1,0:T(8,128)(2,1)S(1)}, u32[]{:S(2)}, u32[]{:S(2)}) collective-permute-start(bf16[256,32]{1,0:T(8,128)(2,1)S(1)} %get-tuple-element.109), channel_id=1, source_target_pairs={{0,4},{4,8},{8,12},{12,16},{16,20},{20,24},{24,28},{28,0},{1,5},{5... | collective-permute-start | bytes 49160 | tf_op jit(solution)/shard_map/while/body/eval_jaxpr/ppermute | solution.py:9
  44.7 5.3 %collective-permute-start.1 = (bf16[256,128]{1,0:T(8,128)(2,1)S(1)}, bf16[256,128]{1,0:T(8,128)(2,1)S(1)}, u32[]{:S(2)}, u32[]{:S(2)}) collective-permute-start(bf16[256,128]{1,0:T(8,128)(2,1)S(1)} %get-tuple-element.110), channel_id=1, source_target_pairs={{0,4},{4,8},{8,12},{12,16},{16,20},{20,24},{24,28},{28,0},{1,5},{5... | collective-permute-start | bytes 196616 | tf_op jit(solution)/shard_map/while/body/eval_jaxpr/ppermute | solution.py:9
  50.9 4.6 %collective-permute-start = (bf16[256,32]{1,0:T(8,128)(2,1)S(1)}, bf16[256,32]{1,0:T(8,128)(2,1)S(1)}, u32[]{:S(2)}, u32[]{:S(2)}) collective-permute-start(bf16[256,32]{1,0:T(8,128)(2,1)S(1)} %get-tuple-element.109), channel_id=1, source_target_pairs={{0,4},{4,8},{8,12},{12,16},{16,20},{20,24},{24,28},{28,0},{1,5},{5... | collective-permute-start | bytes 49160 | tf_op jit(solution)/shard_map/while/body/eval_jaxpr/ppermute | solution.py:9
  51.0 5.3 %collective-permute-start.1 = (bf16[256,128]{1,0:T(8,128)(2,1)S(1)}, bf16[256,128]{1,0:T(8,128)(2,1)S(1)}, u32[]{:S(2)}, u32[]{:S(2)}) collective-permute-start(bf16[256,128]{1,0:T(8,128)(2,1)S(1)} %get-tuple-element.110), channel_id=1, source_target_pairs={{0,4},{4,8},{8,12},{12,16},{16,20},{20,24},{24,28},{28,0},{1,5},{5... | collective-permute-start | bytes 196616 | tf_op jit(solution)/shard_map/while/body/eval_jaxpr/ppermute | solution.py:9
  57.2 4.6 %collective-permute-start = (bf16[256,32]{1,0:T(8,128)(2,1)S(1)}, bf16[256,32]{1,0:T(8,128)(2,1)S(1)}, u32[]{:S(2)}, u32[]{:S(2)}) collective-permute-start(bf16[256,32]{1,0:T(8,128)(2,1)S(1)} %get-tuple-element.109), channel_id=1, source_target_pairs={{0,4},{4,8},{8,12},{12,16},{16,20},{20,24},{24,28},{28,0},{1,5},{5... | collective-permute-start | bytes 49160 | tf_op jit(solution)/shard_map/while/body/eval_jaxpr/ppermute | solution.py:9
  57.3 5.3 %collective-permute-start.1 = (bf16[256,128]{1,0:T(8,128)(2,1)S(1)}, bf16[256,128]{1,0:T(8,128)(2,1)S(1)}, u32[]{:S(2)}, u32[]{:S(2)}) collective-permute-start(bf16[256,128]{1,0:T(8,128)(2,1)S(1)} %get-tuple-element.110), channel_id=1, source_target_pairs={{0,4},{4,8},{8,12},{12,16},{16,20},{20,24},{24,28},{28,0},{1,5},{5... | collective-permute-start | bytes 196616 | tf_op jit(solution)/shard_map/while/body/eval_jaxpr/ppermute | solution.py:9
  63.5 4.6 %collective-permute-start = (bf16[256,32]{1,0:T(8,128)(2,1)S(1)}, bf16[256,32]{1,0:T(8,128)(2,1)S(1)}, u32[]{:S(2)}, u32[]{:S(2)}) collective-permute-start(bf16[256,32]{1,0:T(8,128)(2,1)S(1)} %get-tuple-element.109), channel_id=1, source_target_pairs={{0,4},{4,8},{8,12},{12,16},{16,20},{20,24},{24,28},{28,0},{1,5},{5... | collective-permute-start | bytes 49160 | tf_op jit(solution)/shard_map/while/body/eval_jaxpr/ppermute | solution.py:9
  63.6 5.3 %collective-permute-start.1 = (bf16[256,128]{1,0:T(8,128)(2,1)S(1)}, bf16[256,128]{1,0:T(8,128)(2,1)S(1)}, u32[]{:S(2)}, u32[]{:S(2)}) collective-permute-start(bf16[256,128]{1,0:T(8,128)(2,1)S(1)} %get-tuple-element.110), channel_id=1, source_target_pairs={{0,4},{4,8},{8,12},{12,16},{16,20},{20,24},{24,28},{28,0},{1,5},{5... | collective-permute-start | bytes 196616 | tf_op jit(solution)/shard_map/while/body/eval_jaxpr/ppermute | solution.py:9
  69.8 0.8 copy-start.1
  69.8 23.4 %copy-start.2 = (f32[256,128]{1,0:T(8,128)S(1)}, f32[256,128]{1,0:T(8,128)}, u32[]{:S(2)}) copy-start(f32[256,128]{1,0:T(8,128)} %param.12) | copy-start | bytes 393220
  71.3 61.3 %copy-start.3 = (f32[256,128]{1,0:T(8,128)S(1)}, f32[256,128]{1,0:T(8,128)}, u32[]{:S(2)}) copy-start(f32[256,128]{1,0:T(8,128)} %param.11) | copy-start | bytes 393220
Sparse Core Ops, SparseCore 0:
  70.8 22.4 reduce-scatter.1
where the time goes:
time: 141 us; the launch traced here: 140 us
  waiting for transfers between devices  55.4 us (39%)
  blocking collectives  54 us (38%)
  between operations  14.7 us (10%)
  matrix products  7.59 us (5%)
  starting transfers between devices  3.02 us (2%)
  other arithmetic  2.87 us (2%)
  local copies, waits for them, and re-layouts  2.4 us (2%)
    psum x1, blocking collectives, on_device(): lax.psum((jnp.sum(residual * residual, axis=0), jnp.sum(direction * kerne...  38.4 us
    ppermute x14, waiting for transfers between devices, shifted(): return lax.ppermute(x, axis, [(i, (i + by) % count) for i in range(count)])  33.5 us
    reduce_scatter x1, waiting for transfers between devices, on_device(): lax.psum_scatter(result[2], 'wide', scatter_dimension=0, tiled=True)  22 us
    all_gather x1, blocking collectives, on_device(): lax.all_gather(scaled, 'wide', axis=0, tiled=True)  15.7 us
    dot_general x7, matrix products, direct_turn(): jnp.dot(kernel_block, piece_p, preferred_element_type=jnp.float32)  6.66 us
    ppermute x14, starting transfers between devices, shifted(): return lax.ppermute(x, axis, [(i, (i + by) % count) for i in range(count)])  2.98 us
  transfers between devices with their start and end apart: 15, of which 15 were waited for; matrix products, arithmetic and copies ran while one was open for 1% of the time, Pallas kernels for 0%

commit v1 on v0

v1 whole, which is shorter than its diff:
```python
import functools
import math

import jax
import jax.numpy as jnp
from jax import lax
from jax.experimental import pallas as pl
from jax.experimental.pallas import tpu as pltpu
from jax.sharding import PartitionSpec as P

LN2 = math.log(2.0)
SCALE = 5.0 / (LN2 * LN2)
MESH = pl.DeviceIdType.MESH
TAIL = 16


def rounded(x):
    return x.astype(jnp.bfloat16).astype(jnp.float32)


def three_parts(x):
    high = rounded(x)
    rest = x - high
    middle = rounded(rest)
    return high, middle, rounded(rest - middle)


def matern(scaled_dist):
    dist = jnp.maximum(scaled_dist, 1e-30)
    root = dist * lax.rsqrt(dist)
    poly = 1.0 + root * (LN2 + (LN2 * LN2 / 3.0) * root)
    return (poly * jnp.exp2(-root)).astype(jnp.bfloat16)


def kernel(nb, nw, points, inv_length, noise_var, residual, direction, image, coef,
           feat, feat_z, rows_x, kmat, low_dir, part, part_in, stat, stat_z, stat_b, stat_o,
           fs, fr, fzs, fzr, ps, pr, qs, qr, zs, zr, bs, br):
    b = lax.axis_index("blk")
    w = lax.axis_index("wide")
    chips = nb // 2
    chip, core = b // 2, b % 2
    piece, features = points.shape

    def same_core(q):
        return (lax.rem(chip + q, chips) * 2 + core, w)

    sibling = (chip * 2 + 1 - core, w)

    def along(q):
        return (b, lax.rem(w + q, nw))

    def plane(slot):
        return (lax.rem(chip + slot // 2, chips) * 2 + (core if slot % 2 == 0 else 1 - core), w)

    def back(slot):
        return (chips - slot // 2) % chips * 2 + slot % 2

    barrier = pltpu.get_barrier_semaphore()
    for slot in range(1, nb):
        pl.semaphore_signal(barrier, inc=1, device_id=plane(slot), device_id_type=MESH)
    for q in range(1, nw):
        pl.semaphore_signal(barrier, inc=1, device_id=along(q), device_id_type=MESH)

    def copy(src, dst, send, recv, to):
        return pltpu.make_async_remote_copy(
            src_ref=src, dst_ref=dst, send_sem=send, recv_sem=recv, device_id=to, device_id_type=MESH
        )

    scaled = rounded(points[...].astype(jnp.float32) * inv_length[...])
    wide = jnp.concatenate([scaled, jnp.zeros((piece, 128 - features), jnp.float32)], axis=1)
    x_t = wide.T[:features]
    s1, s2, s3 = three_parts(SCALE * jnp.sum(x_t * x_t, axis=0, keepdims=True))
    row = lax.broadcasted_iota(jnp.int32, (TAIL, piece), 0)
    tail = jnp.where((row >= 3) & (row <= 10), 1.0, 0.0)
    tail = jnp.where((row >= 6) & (row <= 7), 0.0, tail)
    for at, value in ((0, s1), (1, s2), (2, s3), (11, s1), (12, s2), (13, s3)):
        tail = jnp.where(row == at, value, tail)
    feat[0] = jnp.concatenate([x_t, tail], axis=0).astype(jnp.bfloat16)
    low_dir[0:piece] = direction[...].astype(jnp.bfloat16)
    pl.semaphore_wait(barrier, nb - 1 + nw - 1)

    sends = []

    def go(c):
        c.start()
        sends.append(c)
        return c

    def feat_copy(src_slot, dst_slot, to):
        return copy(feat.at[src_slot], feat.at[dst_slot], fs.at[dst_slot], fr.at[dst_slot], to)

    def dir_copy(src_slot, dst_slot, to):
        return copy(low_dir.at[pl.ds(src_slot * piece, piece)], low_dir.at[pl.ds(dst_slot * piece, piece)],
                    ps.at[dst_slot], pr.at[dst_slot], to)

    for q in range(1, nw):
        go(copy(feat.at[0], feat_z.at[nw - q], fzs.at[q], fzr.at[nw - q], along(q)))
    go(feat_copy(0, 1, sibling))
    for q in range(1, chips):
        go(feat_copy(0, 2 * (chips - q), same_core(q)))
    for q in range(1, chips):
        go(dir_copy(0, 2 * (chips - q), same_core(q)))
    go(dir_copy(0, 1, sibling))

    def feat_arrived(slot):
        feat_copy(slot, slot, sibling).wait_recv()

    def dir_arrived(slot):
        dir_copy(slot, slot, sibling).wait_recv()

    def as_rows(block):
        block = block.astype(jnp.float32)
        x = block[:features]
        h, m, l = three_parts(SCALE * x)
        lanes = jnp.concatenate(
            [-2.0 * h, -2.0 * m, -2.0 * l, block[features + 8 :],
             jnp.zeros((TAIL + 8, piece), jnp.float32)], axis=0)
        return lanes.T.astype(jnp.bfloat16)

    rows_x[0:piece] = as_rows(feat[0])
    for q in range(1, nw):
        copy(feat_z.at[q], feat_z.at[q], fzs.at[q], fzr.at[q], along(q)).wait_recv()
        rows_x[q * piece : (q + 1) * piece] = as_rows(feat_z[q])

    depth = rows_x.shape[1]

    def tiles(slot):
        block = feat[slot]
        cols = jnp.concatenate(
            [block[:features]] * 3 + [block[features:],
             jnp.zeros((depth - 3 * features - TAIL, piece), jnp.bfloat16)], axis=0)

        def body(i, carry):
            at = pl.ds(pl.multiple_of(i * piece, piece), piece)
            dist = jnp.dot(rows_x[at, :], cols, preferred_element_type=jnp.float32)
            kmat[at, slot * piece : (slot + 1) * piece] = matern(dist)
            return carry

        lax.fori_loop(0, nw, body, 0, unroll=nw <= 4)

    for slot in range(nb):
        if slot > 0:
            feat_arrived(slot)
        if slot % 2 == 0:
            if slot > 0:
                go(feat_copy(slot, slot + 1, sibling))
        tiles(slot)
        if slot % 2 == 1 and slot >= nb - 5 and slot >= 3:
            pass
    for q in range(1, chips):
        dir_arrived(2 * q)
        go(dir_copy(2 * q, 2 * q + 1, sibling))
    for q in range(chips):
        dir_arrived(2 * q + 1)

    def partial(q):
        return jnp.dot(kmat[q * piece : (q + 1) * piece, :], low_dir[...],
                       preferred_element_type=jnp.float32)

    for q in range(1, nw):
        part[q] = partial(q).astype(jnp.bfloat16)
        go(copy(part.at[q], part_in.at[nw - q], qs.at[q], qr.at[nw - q], along(q)))
    total = partial(0) + noise_var[...] * direction[...]
    for q in range(1, nw):
        copy(part.at[q], part_in.at[q], qs.at[q], qr.at[q], along(q)).wait_recv()
        total = total + part_in[q].astype(jnp.float32)
    image[...] = total

    def column_sum(x):
        return jnp.sum(x, axis=0, keepdims=True)

    res, direc = residual[...], direction[...]
    at = lax.broadcasted_iota(jnp.int32, (8, res.shape[1]), 0)
    sums = jnp.zeros(at.shape, jnp.float32)
    for k, value in enumerate((res * res, direc * total, res * total, total * total)):
        sums = jnp.where(at == k, column_sum(value), sums)
    stat[...] = sums
    for q in range(1, nw):
        go(copy(stat, stat_z.at[nw - q], zs.at[q], zr.at[nw - q], along(q)))
    for q in range(1, nw):
        copy(stat, stat_z.at[q], zs.at[q], zr.at[q], along(q)).wait_recv()
        sums = sums + stat_z[q]
    stat_o[...] = sums
    for slot in range(1, nb):
        go(copy(stat_o, stat_b.at[back(slot)], bs.at[slot], br.at[back(slot)], plane(slot)))
    for slot in range(1, nb):
        copy(stat_o, stat_b.at[slot], bs.at[slot], br.at[slot], plane(slot)).wait_recv()
        sums = sums + stat_b[slot]
    coef[...] = sums
    for c in sends:
        c.wait_send()


def on_device(nb, nw, points, inv_length, noise_var, solution, residual, direction):
    piece, features = points.shape
    rhs = direction.shape[1]
    vmem = pl.BlockSpec(memory_space=pltpu.VMEM)
    dma = pltpu.SemaphoreType.DMA
    depth = 3 * features + 2 * TAIL
    image, coef = pl.pallas_call(
        functools.partial(kernel, nb, nw),
        out_shape=(
            jax.ShapeDtypeStruct((piece, rhs), jnp.float32),
            jax.ShapeDtypeStruct((8, rhs), jnp.float32),
        ),
        in_specs=[vmem] * 5,
        out_specs=(vmem, vmem),
        scratch_shapes=[
            pltpu.VMEM((nb, features + TAIL, piece), jnp.bfloat16),
            pltpu.VMEM((nw, features + TAIL, piece), jnp.bfloat16),
            pltpu.VMEM((nw * piece, depth), jnp.bfloat16),
            pltpu.VMEM((nw * piece, nb * piece), jnp.bfloat16),
            pltpu.VMEM((nb * piece, rhs), jnp.bfloat16),
            pltpu.VMEM((nw, piece, rhs), jnp.bfloat16),
            pltpu.VMEM((nw, piece, rhs), jnp.bfloat16),
            pltpu.VMEM((8, rhs), jnp.float32),
            pltpu.VMEM((nw, 8, rhs), jnp.float32),
            pltpu.VMEM((nb, 8, rhs), jnp.float32),
            pltpu.VMEM((8, rhs), jnp.float32),
            dma((nb,)), dma((nb,)), dma((nw,)), dma((nw,)), dma((nb,)), dma((nb,)),
            dma((nw,)), dma((nw,)), dma((nw,)), dma((nw,)), dma((nb,)), dma((nb,)),
        ],
        compiler_params=pltpu.CompilerParams(
            collective_id=0, has_side_effects=True, vmem_limit_bytes=60 * 1024 * 1024
        ),
    )(points, inv_length.reshape(1, features), noise_var.reshape(1, 1), residual, direction)
    old_norm, curvature, cross_term, image_norm = coef[0], coef[1], coef[2], coef[3]
    step_length = old_norm / curvature
    new_residual = residual - step_length * image
    new_norm = old_norm - 2.0 * step_length * cross_term + step_length * step_length * image_norm
    new_solution = solution + step_length * direction
    new_direction = new_residual + new_norm / old_norm * direction
    return (new_solution, new_residual, new_direction)


def solution(mesh):
    spec = P(("blk", "wide"), None)
    return jax.shard_map(
        functools.partial(on_device, mesh.shape["blk"], mesh.shape["wide"]),
        mesh=mesh,
        in_specs=(spec, P(), P(), spec, spec, spec),
        out_specs=(spec, spec, spec),
        check_vma=False,
    )
```

time: 141 us -> 38.7 us (0.27)
  waiting for transfers between devices: 55.4 us -> 0 us
  blocking collectives: 54 us -> 0 us
  Pallas kernels: 0 us -> 33.1 us
  between operations: 14.7 us -> 1.31 us
  matrix products: 7.59 us -> 0 us
  starting transfers between devices: 3.02 us -> 0 us
    psum x1 -> x0, blocking collectives: 38.4 us -> none  [on_device(): lax.psum((jnp.sum(residual * residual, axis=0), jnp.sum(direction * kerne...]
    ppermute x14 -> x0, waiting for transfers between devices: 33.5 us -> none  [shifted(): return lax.ppermute(x, axis, [(i, (i + by) % count) for i in range(count)])]
    pallas_call x0 -> x1, Pallas kernels: none -> 33.1 us  [on_device(): pl.pallas_call(functools.partial(kernel, nb, nw), out_shape=(jax.ShapeDty...]
    reduce_scatter x1 -> x0, waiting for transfers between devices: 22 us -> none  [on_device(): lax.psum_scatter(result[2], 'wide', scatter_dimension=0, tiled=True)]
    all_gather x1 -> x0, blocking collectives: 15.7 us -> none  [on_device(): lax.all_gather(scaled, 'wide', axis=0, tiled=True)]
    dot_general x8 -> x0, matrix products: 7.59 us -> none  [the longest x7 6.66 us: direct_turn(): jnp.dot(kernel_block, piece_p, preferred_element_type=jnp.float32)]
    ppermute x14 -> x0, starting transfers between devices: 2.98 us -> none  [shifted(): return lax.ppermute(x, axis, [(i, (i + by) % count) for i in range(count)])]
    reduce_sum x10 -> x0, other arithmetic: 2.08 us -> none  [the longest x9 1.11 us: squares_of(): return jnp.sum(wide_values * wide_values, axis=1)]
  transfers between devices with their start and end apart: 15 -> 0, of which waited for: 15 -> 0; matrix products, arithmetic and copies ran while one was open for 1% -> 0% of each run, Pallas kernels for 0% -> 0%
where the time goes in v1:
time: 38.7 us; the launch traced here: 38.4 us
  Pallas kernels  33.1 us (86%)
  other arithmetic  2.51 us (6%)
  local copies, waits for them, and re-layouts  1.5 us (4%)
  between operations  1.31 us (3%)
    pallas_call x1, Pallas kernels, on_device(): pl.pallas_call(functools.partial(kernel, nb, nw), out_shape=(jax.ShapeDty...  33.1 us
    add x1, other arithmetic, on_device(): new_direction = new_residual + new_norm / old_norm * direction  1.67 us
    unnamed x7, local copies, waits for them, and re-layouts  1.5 us
    mul x1, other arithmetic, on_device(): new_direction = new_residual + new_norm / old_norm * direction  0.83 us

profile of v1, /device:TPU:0, one launch (start us, length us, event | category | flops | bytes accessed | tf_op | source)
XLA Modules:
  0.0 38.4 jit_solution(14858739432429159125)
XLA Ops:
  1.3 0.0 copy-start.2
  1.3 1.5 %copy.9.points = bf16[256,32]{1,0:T(8,128)(2,1)} copy(bf16[256,32]{0,1:T(8,128)(2,1)} %param.6) | data formatting | bytes 32768 | tf_op args[0]
  2.8 0.0 copy-start
  2.8 0.0 copy-start.1
  2.8 33.1 %shard_map.85 = (f32[256,128]{1,0:T(8,128)}, f32[8,128]{1,0:T(8,128)}) custom-call(bf16[256,32]{1,0:T(8,128)(2,1)} %copy.9.points, f32[1,32]{1,0:T(1,128)} %bitcast.7, f32[1,1]{1,0:T(1,128)} %bitcast.5.noise_var, f32[256,128]{1,0:T(8,128)} %residual.1, f32[256,128]{1,0:T(8,128)} %direction.1), custom_call_target="tpu_custom_call" | custom-call | tf_op jit(solution)/shard_map/pallas_call | solution.py:200
  35.9 0.8 %fusion = (f32[128]{0:T(128)S(1)}, f32[1,128]{1,0:T(1,128)S(1)}) fusion(f32[8,128]{1,0:T(8,128)} %get-tuple-element.5), kind=kLoop, calls=%fused_computation.5 | loop fusion | flops 1024 | bytes 3072 | tf_op jit(solution)/shard_map/mul | solution.py:232
  36.7 0.0 copy-done.2
  36.7 0.0 copy-done
  36.7 0.0 copy-done.1
  36.7 1.7 %multiply_add_fusion = (f32[256,128]{1,0:T(8,128)}, f32[256,128]{1,0:T(8,128)}, f32[256,128]{1,0:T(8,128)}) fusion(f32[256,128]{1,0:T(8,128)S(1)} %copy-done, f32[128]{0:T(128)S(1)} %get-tuple-element.9, f32[256,128]{1,0:T(8,128)S(1)} %copy-done.1, f32[256,128]{1,0:T(8,128)} %get-tuple-element.6, f32[128]{0:T(128)S(1)} %bitcast.6, f32[256,128]{1,0:T(8,128)S(1)} %copy-done.2), kind=kLoop, calls=%fused_computation | loop fusion | flops 196608 | bytes 918528 | tf_op jit(solution)/shard_map/add | solution.py:232
Async XLA Ops:
  1.3 35.4 %copy-start.2 = (f32[256,128]{1,0:T(8,128)S(1)}, f32[256,128]{1,0:T(8,128)}, u32[]{:S(2)}) copy-start(f32[256,128]{1,0:T(8,128)} %param.9) | copy-start | bytes 393220
  2.8 33.9 %copy-start = (f32[256,128]{1,0:T(8,128)S(1)}, f32[256,128]{1,0:T(8,128)}, u32[]{:S(2)}) copy-start(f32[256,128]{1,0:T(8,128)} %direction.1) | copy-start | bytes 393220
  2.8 33.9 %copy-start.1 = (f32[256,128]{1,0:T(8,128)S(1)}, f32[256,128]{1,0:T(8,128)}, u32[]{:S(2)}) copy-start(f32[256,128]{1,0:T(8,128)} %residual.1) | copy-start | bytes 393220

commit v2 on v1

--- a/solution.py
+++ b/solution.py
@@ -32,14 +32,14 @@
     return (poly * jnp.exp2(-root)).astype(jnp.bfloat16)
 
 
-def kernel(nb, nw, points, inv_length, noise_var, residual, direction, image, coef,
-           feat, feat_z, rows_x, kmat, low_dir, part, part_in, stat, stat_z, stat_b, stat_o,
+def kernel(nb, nw, points_in, inv_in, noise_in, residual_in, direction_in, image_out, step_out, ratio_out,
+           points, inv_length, noise_var, residual, direction, image, io, feat, feat_z, rows_x, kmat, low_dir, part, part_in, stat, stat_z, stat_b, stat_o,
            fs, fr, fzs, fzr, ps, pr, qs, qr, zs, zr, bs, br):
     b = lax.axis_index("blk")
     w = lax.axis_index("wide")
     chips = nb // 2
     chip, core = b // 2, b % 2
-    piece, features = points.shape
+    features, piece = points.shape
 
     def same_core(q):
         return (lax.rem(chip + q, chips) * 2 + core, w)
@@ -66,9 +66,22 @@
             src_ref=src, dst_ref=dst, send_sem=send, recv_sem=recv, device_id=to, device_id_type=MESH
         )
 
-    scaled = rounded(points[...].astype(jnp.float32) * inv_length[...])
-    wide = jnp.concatenate([scaled, jnp.zeros((piece, 128 - features), jnp.float32)], axis=1)
-    x_t = wide.T[:features]
+    loads = [
+        pltpu.make_async_copy(src, dst, io.at[k])
+        for k, (src, dst) in enumerate(
+            ((points_in, points), (inv_in, inv_length), (direction_in, direction),
+             (noise_in, noise_var), (residual_in, residual))
+        )
+    ]
+    for load in loads:
+        load.start()
+    for load in loads[:2]:
+        load.wait()
+
+    inv_row = jnp.concatenate(
+        [inv_length[...], jnp.zeros((1, 128 - features), jnp.float32)], axis=1)
+    inv_column = jnp.broadcast_to(inv_row, (8, 128)).T[:features, 0:1]
+    x_t = rounded(points[...].astype(jnp.float32) * inv_column)
     s1, s2, s3 = three_parts(SCALE * jnp.sum(x_t * x_t, axis=0, keepdims=True))
     row = lax.broadcasted_iota(jnp.int32, (TAIL, piece), 0)
     tail = jnp.where((row >= 3) & (row <= 10), 1.0, 0.0)
@@ -76,6 +89,8 @@
     for at, value in ((0, s1), (1, s2), (2, s3), (11, s1), (12, s2), (13, s3)):
         tail = jnp.where(row == at, value, tail)
     feat[0] = jnp.concatenate([x_t, tail], axis=0).astype(jnp.bfloat16)
+    for load in loads[2:]:
+        load.wait()
     low_dir[0:piece] = direction[...].astype(jnp.bfloat16)
     pl.semaphore_wait(barrier, nb - 1 + nw - 1)
 
@@ -117,39 +132,58 @@
              jnp.zeros((TAIL + 8, piece), jnp.float32)], axis=0)
         return lanes.T.astype(jnp.bfloat16)
 
-    rows_x[0:piece] = as_rows(feat[0])
-    for q in range(1, nw):
-        copy(feat_z.at[q], feat_z.at[q], fzs.at[q], fzr.at[q], along(q)).wait_recv()
-        rows_x[q * piece : (q + 1) * piece] = as_rows(feat_z[q])
-
     depth = rows_x.shape[1]
 
-    def tiles(slot):
+    def tile(at, slot):
         block = feat[slot]
         cols = jnp.concatenate(
             [block[:features]] * 3 + [block[features:],
              jnp.zeros((depth - 3 * features - TAIL, piece), jnp.bfloat16)], axis=0)
-
-        def body(i, carry):
-            at = pl.ds(pl.multiple_of(i * piece, piece), piece)
-            dist = jnp.dot(rows_x[at, :], cols, preferred_element_type=jnp.float32)
-            kmat[at, slot * piece : (slot + 1) * piece] = matern(dist)
-            return carry
-
-        lax.fori_loop(0, nw, body, 0, unroll=nw <= 4)
-
-    for slot in range(nb):
-        if slot > 0:
-            feat_arrived(slot)
-        if slot % 2 == 0:
-            if slot > 0:
-                go(feat_copy(slot, slot + 1, sibling))
-        tiles(slot)
-        if slot % 2 == 1 and slot >= nb - 5 and slot >= 3:
-            pass
-    for q in range(1, chips):
+        dist = jnp.dot(rows_x[at, :], cols, preferred_element_type=jnp.float32)
+        kmat[at, slot * piece : (slot + 1) * piece] = matern(dist)
+
+    def feat_z_arrived(q):
+        copy(feat_z.at[q], feat_z.at[q], fzs.at[q], fzr.at[q], along(q)).wait_recv()
+
+    def relay_direction(q):
         dir_arrived(2 * q)
         go(dir_copy(2 * q, 2 * q + 1, sibling))
+
+    rows_x[0:piece] = as_rows(feat[0])
+    tile(pl.ds(0, piece), 0)
+    feat_arrived(1)
+    tile(pl.ds(0, piece), 1)
+    for q in range(1, chips):
+        feat_arrived(2 * q)
+        go(feat_copy(2 * q, 2 * q + 1, sibling))
+        tile(pl.ds(0, piece), 2 * q)
+    for q in range(1, chips):
+        feat_arrived(2 * q + 1)
+        tile(pl.ds(0, piece), 2 * q + 1)
+    if nw <= 4:
+        relayed = 1
+        for q in range(1, nw):
+            feat_z_arrived(q)
+            rows_x[q * piece : (q + 1) * piece] = as_rows(feat_z[q])
+            for slot in range(nb):
+                tile(pl.ds(q * piece, piece), slot)
+                if q == nw - 1 and slot in (0, nb // 2) and relayed < chips:
+                    relay_direction(relayed)
+                    relayed += 1
+    else:
+        relayed = 1
+        for q in range(1, nw):
+            feat_z_arrived(q)
+            rows_x[q * piece : (q + 1) * piece] = as_rows(feat_z[q])
+
+        def row_tiles(q, carry):
+            for slot in range(nb):
+                tile(pl.ds(pl.multiple_of(q * piece, piece), piece), slot)
+            return carry
+
+        lax.fori_loop(1, nw, row_tiles, 0)
+    for q in range(relayed, chips):
+        relay_direction(q)
     for q in range(chips):
         dir_arrived(2 * q + 1)
 
@@ -165,6 +199,8 @@
         copy(part.at[q], part_in.at[q], qs.at[q], qr.at[q], along(q)).wait_recv()
         total = total + part_in[q].astype(jnp.float32)
     image[...] = total
+    store = pltpu.make_async_copy(image, image_out, io.at[5])
+    store.start()
 
     def column_sum(x):
         return jnp.sum(x, axis=0, keepdims=True)
@@ -186,7 +222,11 @@
     for slot in range(1, nb):
         copy(stat_o, stat_b.at[slot], bs.at[slot], br.at[slot], plane(slot)).wait_recv()
         sums = sums + stat_b[slot]
-    coef[...] = sums
+    old_norm, step = sums[0:1], sums[0:1] / sums[1:2]
+    new_norm = old_norm - 2.0 * step * sums[2:3] + step * step * sums[3:4]
+    step_out[...] = step
+    ratio_out[...] = new_norm / old_norm
+    store.wait()
     for c in sends:
         c.wait_send()
 
@@ -195,17 +235,26 @@
     piece, features = points.shape
     rhs = direction.shape[1]
     vmem = pl.BlockSpec(memory_space=pltpu.VMEM)
+    hbm = pl.BlockSpec(memory_space=pl.ANY)
     dma = pltpu.SemaphoreType.DMA
     depth = 3 * features + 2 * TAIL
-    image, coef = pl.pallas_call(
+    image, step_length, ratio = pl.pallas_call(
         functools.partial(kernel, nb, nw),
         out_shape=(
             jax.ShapeDtypeStruct((piece, rhs), jnp.float32),
-            jax.ShapeDtypeStruct((8, rhs), jnp.float32),
+            jax.ShapeDtypeStruct((1, rhs), jnp.float32),
+            jax.ShapeDtypeStruct((1, rhs), jnp.float32),
         ),
-        in_specs=[vmem] * 5,
-        out_specs=(vmem, vmem),
+        in_specs=[hbm] * 5,
+        out_specs=(hbm, vmem, vmem),
         scratch_shapes=[
+            pltpu.VMEM((features, piece), points.dtype),
+            pltpu.VMEM((1, features), jnp.float32),
+            pltpu.VMEM((1, 1), jnp.float32),
+            pltpu.VMEM((piece, rhs), jnp.float32),
+            pltpu.VMEM((piece, rhs), jnp.float32),
+            pltpu.VMEM((piece, rhs), jnp.float32),
+            dma((6,)),
             pltpu.VMEM((nb, features + TAIL, piece), jnp.bfloat16),
             pltpu.VMEM((nw, features + TAIL, piece), jnp.bfloat16),
             pltpu.VMEM((nw * piece, depth), jnp.bfloat16),
@@ -223,13 +272,10 @@
         compiler_params=pltpu.CompilerParams(
             collective_id=0, has_side_effects=True, vmem_limit_bytes=60 * 1024 * 1024
         ),
-    )(points, inv_length.reshape(1, features), noise_var.reshape(1, 1), residual, direction)
-    old_norm, curvature, cross_term, image_norm = coef[0], coef[1], coef[2], coef[3]
-    step_length = old_norm / curvature
+    )(points.T, inv_length.reshape(1, features), noise_var.reshape(1, 1), residual, direction)
     new_residual = residual - step_length * image
-    new_norm = old_norm - 2.0 * step_length * cross_term + step_length * step_length * image_norm
     new_solution = solution + step_length * direction
-    new_direction = new_residual + new_norm / old_norm * direction
+    new_direction = new_residual + ratio * direction
     return (new_solution, new_residual, new_direction)
 
 

time: 38.7 us -> 35.4 us (0.915)
  Pallas kernels: 33.1 us -> 31.5 us
  local copies, waits for them, and re-layouts: 1.5 us -> 0.62 us
  other arithmetic: 2.51 us -> 1.73 us
    pallas_call x1, Pallas kernels: 33.1 us -> 31.5 us  [on_device(): pl.pallas_call(functools.partial(kernel, nb, nw), out_shape=(jax.ShapeDty...]
    unnamed x7 -> x8, local copies, waits for them, and re-layouts: 1.5 us -> 0.62 us
    mul x1 -> x0, other arithmetic: 0.83 us -> none  [on_device(): new_direction = new_residual + new_norm / old_norm * direction]
where the time goes in v2:
time: 35.4 us; the launch traced here: 35.2 us
  Pallas kernels  31.5 us (89%)
  other arithmetic  1.73 us (5%)
  between operations  1.33 us (4%)
  local copies, waits for them, and re-layouts  0.62 us (2%)
    pallas_call x1, Pallas kernels, on_device(): pl.pallas_call(functools.partial(kernel, nb, nw), out_shape=(jax.ShapeDty...  31.5 us
    add x1, other arithmetic, on_device(): new_direction = new_residual + ratio * direction  1.73 us

profile of v2, /device:TPU:0, one launch (start us, length us, event | category | flops | bytes accessed | tf_op | source)
XLA Modules:
  0.0 35.2 jit_solution(13823981828195072681)
XLA Ops:
  1.3 0.0 copy-start
  1.3 0.0 copy-start.1
  1.3 31.5 %shard_map.85 = (f32[256,128]{1,0:T(8,128)}, f32[1,128]{1,0:T(1,128)}, f32[1,128]{1,0:T(1,128)}) custom-call(bf16[32,256]{1,0:T(8,128)(2,1)} %bitcast.6, f32[1,32]{1,0:T(1,128)} %bitcast.7, f32[1,1]{1,0:T(1,128)} %bitcast.5.noise_in, f32[256,128]{1,0:T(8,128)} %residual_in.1, f32[256,128]{1,0:T(8,128)} %direction_in.1), custom_call_target="tpu_custom_call" | custom-call | tf_op jit(solution)/shard_map/pallas_call | solution.py:241
  32.8 0.0 copy-start.2
  32.8 0.0 copy-start.3
  32.8 0.0 copy-done
  32.8 0.0 copy-done.1
  32.8 0.6 %copy-done.2 = f32[1,128]{1,0:T(1,128)S(1)} copy-done((f32[1,128]{1,0:T(1,128)S(1)}, f32[1,128]{1,0:T(1,128)}, u32[]{:S(2)}) %copy-start.2) | copy-done | bytes 536
  33.4 0.0 copy-done.3
  33.4 1.7 %multiply_add_fusion = (f32[256,128]{1,0:T(8,128)}, f32[256,128]{1,0:T(8,128)}, f32[256,128]{1,0:T(8,128)}) fusion(f32[256,128]{1,0:T(8,128)S(1)} %copy-done, f32[128]{0:T(128)S(1)} %bitcast.9, f32[256,128]{1,0:T(8,128)S(1)} %copy-done.1, f32[256,128]{1,0:T(8,128)} %get-tuple-element.7, f32[128]{0:T(128)S(1)} %bitcast.8, f32[256,128]{1,0:T(8,128)} %param.9), kind=kLoop, calls=%fused_computation | loop fusion | flops 196608 | bytes 918528 | tf_op jit(solution)/shard_map/add | solution.py:278
Async XLA Ops:
  1.3 31.5 %copy-start = (f32[256,128]{1,0:T(8,128)S(1)}, f32[256,128]{1,0:T(8,128)}, u32[]{:S(2)}) copy-start(f32[256,128]{1,0:T(8,128)} %direction_in.1) | copy-start | bytes 393220
  1.3 31.5 %copy-start.1 = (f32[256,128]{1,0:T(8,128)S(1)}, f32[256,128]{1,0:T(8,128)}, u32[]{:S(2)}) copy-start(f32[256,128]{1,0:T(8,128)} %residual_in.1) | copy-start | bytes 393220
  32.8 0.6 %copy-start.2 = (f32[1,128]{1,0:T(1,128)S(1)}, f32[1,128]{1,0:T(1,128)}, u32[]{:S(2)}) copy-start(f32[1,128]{1,0:T(1,128)} %get-tuple-element.6) | copy-start | bytes 1540
  32.8 0.6 %copy-start.3 = (f32[1,128]{1,0:T(1,128)S(1)}, f32[1,128]{1,0:T(1,128)}, u32[]{:S(2)}) copy-start(f32[1,128]{1,0:T(1,128)} %get-tuple-element.8) | copy-start | bytes 1540

commit v3 on v2

--- a/solution.py
+++ b/solution.py
@@ -94,6 +94,14 @@
     low_dir[0:piece] = direction[...].astype(jnp.bfloat16)
     pl.semaphore_wait(barrier, nb - 1 + nw - 1)
 
+    upper = lax.div(2 * w, nw)
+
+    def near(k):
+        return k + upper * (nw - 2 * k)
+
+    def rows_at(q):
+        return pl.ds(pl.multiple_of(q * piece, piece), piece)
+
     sends = []
 
     def go(c):
@@ -108,7 +116,8 @@
         return copy(low_dir.at[pl.ds(src_slot * piece, piece)], low_dir.at[pl.ds(dst_slot * piece, piece)],
                     ps.at[dst_slot], pr.at[dst_slot], to)
 
-    for q in range(1, nw):
+    for k in range(1, nw):
+        q = near(nw - k)
         go(copy(feat.at[0], feat_z.at[nw - q], fzs.at[q], fzr.at[nw - q], along(q)))
     go(feat_copy(0, 1, sibling))
     for q in range(1, chips):
@@ -162,12 +171,13 @@
         tile(pl.ds(0, piece), 2 * q + 1)
     if nw <= 4:
         relayed = 1
-        for q in range(1, nw):
+        for k in range(1, nw):
+            q = near(k)
             feat_z_arrived(q)
-            rows_x[q * piece : (q + 1) * piece] = as_rows(feat_z[q])
+            rows_x[rows_at(q), :] = as_rows(feat_z[q])
             for slot in range(nb):
-                tile(pl.ds(q * piece, piece), slot)
-                if q == nw - 1 and slot in (0, nb // 2) and relayed < chips:
+                tile(rows_at(q), slot)
+                if k == nw - 1 and slot in (0, nb // 2) and relayed < chips:
                     relay_direction(relayed)
                     relayed += 1
     else:
@@ -188,10 +198,11 @@
         dir_arrived(2 * q + 1)
 
     def partial(q):
-        return jnp.dot(kmat[q * piece : (q + 1) * piece, :], low_dir[...],
+        return jnp.dot(kmat[rows_at(q), :], low_dir[...],
                        preferred_element_type=jnp.float32)
 
-    for q in range(1, nw):
+    for k in range(1, nw):
+        q = near(nw - k)
         part[q] = partial(q).astype(jnp.bfloat16)
         go(copy(part.at[q], part_in.at[nw - q], qs.at[q], qr.at[nw - q], along(q)))
     total = partial(0) + noise_var[...] * direction[...]

time: 35.4 us -> 34.9 us (0.986)
  Pallas kernels: 31.5 us -> 31 us
    pallas_call x1, Pallas kernels: 31.5 us -> 31 us  [on_device(): pl.pallas_call(functools.partial(kernel, nb, nw), out_shape=(jax.ShapeDty...]
where the time goes in v3:
time: 34.9 us; the launch traced here: 34.7 us
  Pallas kernels  31 us (89%)
  other arithmetic  1.73 us (5%)
  between operations  1.33 us (4%)
  local copies, waits for them, and re-layouts  0.62 us (2%)
    pallas_call x1, Pallas kernels, on_device(): pl.pallas_call(functools.partial(kernel, nb, nw), out_shape=(jax.ShapeDty...  31 us
    add x1, other arithmetic, on_device(): new_direction = new_residual + ratio * direction  1.73 us

profile of v3, /device:TPU:0, one launch (start us, length us, event | category | flops | bytes accessed | tf_op | source)
XLA Modules:
  0.0 34.7 jit_solution(9100170816936021639)
XLA Ops:
  1.3 0.0 copy-start
  1.3 0.0 copy-start.1
  1.3 31.0 %shard_map.85 = (f32[256,128]{1,0:T(8,128)}, f32[1,128]{1,0:T(1,128)}, f32[1,128]{1,0:T(1,128)}) custom-call(bf16[32,256]{1,0:T(8,128)(2,1)} %bitcast.6, f32[1,32]{1,0:T(1,128)} %bitcast.7, f32[1,1]{1,0:T(1,128)} %bitcast.5.noise_in, f32[256,128]{1,0:T(8,128)} %residual_in.1, f32[256,128]{1,0:T(8,128)} %direction_in.1), custom_call_target="tpu_custom_call" | custom-call | tf_op jit(solution)/shard_map/pallas_call | solution.py:252
  32.3 0.0 copy-start.2
  32.3 0.0 copy-start.3
  32.4 0.0 copy-done
  32.4 0.0 copy-done.1
  32.4 0.6 %copy-done.2 = f32[1,128]{1,0:T(1,128)S(1)} copy-done((f32[1,128]{1,0:T(1,128)S(1)}, f32[1,128]{1,0:T(1,128)}, u32[]{:S(2)}) %copy-start.2) | copy-done | bytes 536
  32.9 0.0 copy-done.3
  33.0 1.7 %multiply_add_fusion = (f32[256,128]{1,0:T(8,128)}, f32[256,128]{1,0:T(8,128)}, f32[256,128]{1,0:T(8,128)}) fusion(f32[256,128]{1,0:T(8,128)S(1)} %copy-done, f32[128]{0:T(128)S(1)} %bitcast.9, f32[256,128]{1,0:T(8,128)S(1)} %copy-done.1, f32[256,128]{1,0:T(8,128)} %get-tuple-element.7, f32[128]{0:T(128)S(1)} %bitcast.8, f32[256,128]{1,0:T(8,128)} %param.9), kind=kLoop, calls=%fused_computation | loop fusion | flops 196608 | bytes 918528 | tf_op jit(solution)/shard_map/add | solution.py:289
Async XLA Ops:
  1.3 31.1 %copy-start = (f32[256,128]{1,0:T(8,128)S(1)}, f32[256,128]{1,0:T(8,128)}, u32[]{:S(2)}) copy-start(f32[256,128]{1,0:T(8,128)} %direction_in.1) | copy-start | bytes 393220
  1.3 31.1 %copy-start.1 = (f32[256,128]{1,0:T(8,128)S(1)}, f32[256,128]{1,0:T(8,128)}, u32[]{:S(2)}) copy-start(f32[256,128]{1,0:T(8,128)} %residual_in.1) | copy-start | bytes 393220
  32.3 0.6 %copy-start.2 = (f32[1,128]{1,0:T(1,128)S(1)}, f32[1,128]{1,0:T(1,128)}, u32[]{:S(2)}) copy-start(f32[1,128]{1,0:T(1,128)} %get-tuple-element.6) | copy-start | bytes 1540
  32.3 0.6 %copy-start.3 = (f32[1,128]{1,0:T(1,128)S(1)}, f32[1,128]{1,0:T(1,128)}, u32[]{:S(2)}) copy-start(f32[1,128]{1,0:T(1,128)} %get-tuple-element.8) | copy-start | bytes 1540
